TPU v7x, 32 devices: a whole 2x2x4 slice. The times are simulated.
32 devices in a mesh: samp: 16 (over z, y, x), feat: 2 (over core).
Axes of the slice: x: 2, y: 2, z: 4, core: 2. Of those that a mesh axis runs over, the one named last changes fastest.
Arguments:
- design_matrix: bfloat16 [2048, 32768], P('samp', 'feat'), may hold values from -0.046875 to 0.046875
- labels: int32 [2048], P('samp'), may hold values from 0 to 1
- weights: float32 [16, 32768], P(None, ('feat', 'samp')), may hold values from -6 to 6
- lambdas: float32 [16], replicated, may hold values from 0.05 to 1
- sketch: bfloat16 [32768, 384], P(('feat', 'samp')), may hold values from -0.03125 to 0.03125
- sketch_values: float32 [384], replicated, may hold values from 0.05 to 2
Outputs:
- new_weights: float32 [16, 32768], P(None, ('feat', 'samp'))
All inputs are finite; a program needn't handle non-finite values.
Results may differ from a plain program's by a relative error of at most 0.004.
Values may be sent and summed in bfloat16 or wider, within the bound.
No kernel may reach another device: no remote copies, remote signals or barrier semaphores. Data moves between devices by JAX's collectives and lax.ppermute only.
A program may use at most 64 MiB of HBM per device.

v0:
```python
import jax
import jax.numpy as jnp
from jax import lax
from jax.sharding import PartitionSpec as P

ITERS = 2


def shards(design_matrix, labels, weights, lambdas, sketch, sketch_values):
    sketch_full = sketch.astype(jnp.float32)
    smallest = jnp.min(sketch_values)
    ratios = (smallest + lambdas[:, None]) / (sketch_values[None, :] + lambdas[:, None]) - 1.0

    def apply_rows(vector):
        vector_half = vector.astype(jnp.bfloat16)
        partial_rows = lax.dot_general(
            lax.all_gather(vector_half, "samp", axis=1, tiled=True),
            design_matrix,
            (((1,), (1,)), ((), ())),
            preferred_element_type=jnp.float32,
        )
        return lax.psum(partial_rows, "feat")

    def apply_columns(values):
        return lax.psum_scatter(
            lax.dot_general(
                design_matrix, values, (((0,), (1,)), ((), ())), preferred_element_type=jnp.float32
            ),
            "samp",
            scatter_dimension=0,
            tiled=True,
        ).T

    def precondition(residual):
        projected = jnp.dot(residual, sketch_full, precision=lax.Precision.HIGHEST)
        projected = lax.psum(projected, ("samp", "feat"))
        correction = lax.dot_general(
            ratios * projected,
            sketch_full,
            (((1,), (1,)), ((), ())),
            precision=lax.Precision.HIGHEST,
        )
        precond_res = residual + correction
        res_dot = lax.psum(jnp.sum(residual * precond_res, axis=1), ("samp", "feat"))
        return (precond_res, res_dot)

    logits = apply_rows(weights)
    probability = jax.nn.sigmoid(logits)
    hessian_diag = probability * (1.0 - probability)
    miss_rows = (probability - labels[None, :].astype(jnp.float32)).astype(jnp.bfloat16)
    gradient = apply_columns(miss_rows) + lambdas[:, None] * weights
    residual = -gradient
    precond_res, res_dot = precondition(residual)
    direction = precond_res
    update = jnp.zeros_like(residual)
    for iteration in range(ITERS):
        image_rows = apply_rows(direction)
        hess_dir = (
            apply_columns((hessian_diag * image_rows).astype(jnp.bfloat16))
            + lambdas[:, None] * direction
        )
        curvature = lax.psum(jnp.sum(direction * hess_dir, axis=1), ("samp", "feat"))
        step_size = res_dot / curvature
        update = update + step_size[:, None] * direction
        if iteration + 1 < ITERS:
            residual = residual - step_size[:, None] * hess_dir
            precond_res, new_dot = precondition(residual)
            direction = precond_res + (new_dot / res_dot)[:, None] * direction
            res_dot = new_dot
    return weights + update


def solution(mesh):
    return jax.shard_map(
        shards,
        mesh=mesh,
        in_specs=(
            P("samp", "feat"),
            P("samp"),
            P(None, ("feat", "samp")),
            P(),
            P(("feat", "samp"), None),
            P(),
        ),
        out_specs=P(None, ("feat", "samp")),
        check_vma=False,
    )
```

profile of v0, /device:TPU:10, one launch (start us, length us, event | category | flops | bytes accessed | tf_op | source)
XLA Modules:
  0.0 596.1 jit_solution(18189731865618623638)
XLA Ops:
  6.5 0.0 copy-start
  6.5 0.0 reduce-scatter.4.cloned.1.call-start
  6.5 0.7 convert_element_type.24
  7.3 0.8 convert_element_type.23
  8.1 33.0 %all_gather.9 = bf16[16,16384]{1,0:T(8,128)(2,1)S(1)} all-gather(bf16[16,1024]{1,0:T(8,128)(2,1)S(1)} %convert_element_type.23), channel_id=1, replica_groups=mesh['samp'=16,'feat'=2] {'samp'}, dimensions={1}, use_global_device_ids=true | all-gather | bytes 557056 | tf_op jit(solution)/shard_map/all_gather | solution.py:17
  41.1 3.4 fusion.22
  44.4 0.0 copy-start.3
  44.4 0.0 copy-start.2
  44.4 0.0 copy-start.1
  44.5 2.6 psum.63
  47.1 3.8 convolution_bitcast_fusion.2
  51.0 0.0 reduce-scatter.4.cloned.1.call-update
  51.0 0.0 reduce-scatter.6.cloned.1.call-start
  51.0 0.0 copy-done.3
  51.0 0.6 reduce_min.9
  51.6 0.0 copy-done.2
  51.6 0.6 broadcast_add_fusion
  52.3 73.3 %reduce-scatter.4.cloned.1.call-done = f32[1024,16]{0,1:T(8,128)} async-done(((f32[16384,16]{0,1:T(8,128)}), f32[1024,16]{0,1:T(8,128)}) %reduce-scatter.4.cloned.1.call-update) | async-done | bytes 65552 | tf_op jit(solution)/shard_map/reduce_scatter | solution.py:25
  125.6 0.0 copy-done.1
  125.6 0.9 fusion.2
  126.6 0.0 copy-done
  126.6 0.4 fusion.23
  127.0 50.1 %psum.64 = f32[16,384]{1,0:T(8,128)S(1)} all-reduce(f32[16,384]{1,0:T(8,128)S(1)} %fusion.23), channel_id=1, replica_groups=mesh['samp'=16,'feat'=2] {'samp','feat'}, use_global_device_ids=true, to_apply=%region_3.0 | all-reduce | flops 6144 | bytes 49152 | tf_op jit(solution)/shard_map/psum | solution.py:36
  177.1 0.7 fusion.21
  177.8 32.0 %all_gather.10 = bf16[16,16384]{1,0:T(8,128)(2,1)S(1)} all-gather(bf16[16,1024]{1,0:T(8,128)(2,1)S(1)} %get-tuple-element.9), channel_id=1, replica_groups=mesh['samp'=16,'feat'=2] {'samp'}, dimensions={1}, use_global_device_ids=true | all-gather | bytes 557056 | tf_op jit(solution)/shard_map/all_gather | solution.py:17
  209.8 3.4 fusion.24
  213.1 2.5 psum.66
  215.6 3.8 convolution_bitcast_fusion.1
  219.5 0.0 reduce-scatter.6.cloned.1.call-update
  219.5 0.0 reduce-scatter.8.cloned.1.call-start
  219.5 71.6 %reduce-scatter.6.cloned.1.call-done = f32[1024,16]{0,1:T(8,128)} async-done(((f32[16384,16]{0,1:T(8,128)}), f32[1024,16]{0,1:T(8,128)}) %reduce-scatter.6.cloned.1.call-update) | async-done | bytes 65552 | tf_op jit(solution)/shard_map/reduce_scatter | solution.py:25
  291.1 1.0 multiply_reduce_fusion.1
  292.1 49.7 %all-reduce = (f32[16]{0:T(128)S(1)}, f32[16]{0:T(128)S(1)}) all-reduce(f32[16]{0:T(128)S(1)} %get-tuple-element.6, f32[16]{0:T(128)S(1)} %get-tuple-element.5), channel_id=1, replica_groups=mesh['samp'=16,'feat'=2] {'samp','feat'}, use_global_device_ids=true, to_apply=%region_5.0 | all-reduce | flops 32 | bytes 256 | tf_op jit(solution)/shard_map/psum | solution.py:44
  341.9 0.9 multiply_subtract_fusion
  342.8 0.4 fusion.25
  343.2 38.3 %psum.68 = f32[16,384]{1,0:T(8,128)S(1)} all-reduce(f32[16,384]{1,0:T(8,128)S(1)} %fusion.25), channel_id=1, replica_groups=mesh['samp'=16,'feat'=2] {'samp','feat'}, use_global_device_ids=true, to_apply=%region_10.0 | all-reduce | flops 6144 | bytes 49152 | tf_op jit(solution)/shard_map/psum | solution.py:36
  381.5 0.8 multiply_reduce_fusion
  382.3 41.9 %psum.69 = f32[16]{0:T(128)S(1)} all-reduce(f32[16]{0:T(128)S(1)} %get-tuple-element.11), channel_id=1, replica_groups=mesh['samp'=16,'feat'=2] {'samp','feat'}, use_global_device_ids=true, to_apply=%region_12.0 | all-reduce | flops 16 | bytes 128 | tf_op jit(solution)/shard_map/psum | solution.py:44
  424.2 0.1 fusion.20
  424.3 31.8 %all_gather.11 = bf16[16,16384]{1,0:T(8,128)(2,1)S(1)} all-gather(bf16[16,1024]{1,0:T(8,128)(2,1)S(1)} %fusion.20), channel_id=1, replica_groups=mesh['samp'=16,'feat'=2] {'samp'}, dimensions={1}, use_global_device_ids=true | all-gather | bytes 557056 | tf_op jit(solution)/shard_map/all_gather | solution.py:17
  456.1 3.4 fusion.26
  459.5 2.5 psum.70
  462.0 3.9 convolution_bitcast_fusion
  465.8 0.0 reduce-scatter.8.cloned.1.call-update
  465.8 72.2 %reduce-scatter.8.cloned.1.call-done = f32[1024,16]{0,1:T(8,128)} async-done(((f32[16384,16]{0,1:T(8,128)}), f32[1024,16]{0,1:T(8,128)}) %reduce-scatter.8.cloned.1.call-update) | async-done | bytes 65552 | tf_op jit(solution)/shard_map/reduce_scatter | solution.py:25
  538.1 1.0 fusion.1
  539.1 49.8 %psum.71 = f32[16]{0:T(128)S(1)} all-reduce(f32[16]{0:T(128)S(1)} %fusion.1), channel_id=1, replica_groups=mesh['samp'=16,'feat'=2] {'samp','feat'}, use_global_device_ids=true, to_apply=%region_16.0 | all-reduce | flops 16 | bytes 128 | tf_op jit(solution)/shard_map/psum | solution.py:62
  588.9 0.7 add_add_fusion
  (3 shorter events, 0.0 us)
Async XLA Ops:
  6.5 120.0 %copy-start = (bf16[1024,384]{1,0:T(8,128)(2,1)S(1)}, bf16[1024,384]{1,0:T(8,128)(2,1)}, u32[]{:S(2)}) copy-start(bf16[1024,384]{1,0:T(8,128)(2,1)} %param.10) | copy-start | bytes 2359300
  6.5 119.1 %reduce-scatter.4.cloned.1.call-start = ((), (), s32[]{:S(2)}) async-start(), calls=%async_computation.3 | async-start | bytes 1114112 | tf_op jit(solution)/shard_map/reduce_scatter | solution.py:25
  44.4 6.6 %copy-start.3 = (f32[384]{0:T(512)S(1)}, f32[384]{0:T(512)}, u32[]{:S(2)}) copy-start(f32[384]{0:T(512)} %param.11) | copy-start | bytes 4612
  44.4 7.2 %copy-start.2 = (f32[16]{0:T(128)S(1)}, f32[16]{0:T(128)}, u32[]{:S(2)}) copy-start(f32[16]{0:T(128)} %param.9) | copy-start | bytes 196
  44.4 81.2 %copy-start.1 = (f32[16,1024]{1,0:T(8,128)S(1)}, f32[16,1024]{1,0:T(8,128)}, u32[]{:S(2)}) copy-start(f32[16,1024]{1,0:T(8,128)} %param.8) | copy-start | bytes 196612
  51.0 240.1 %reduce-scatter.6.cloned.1.call-start = ((), (), s32[]{:S(2)}) async-start(), calls=%async_computation.4 | async-start | bytes 1114112 | tf_op jit(solution)/shard_map/reduce_scatter | solution.py:25
  219.5 318.6 %reduce-scatter.8.cloned.1.call-start = ((), (), s32[]{:S(2)}) async-start(), calls=%async_computation.5 | async-start | bytes 1114112 | tf_op jit(solution)/shard_map/reduce_scatter | solution.py:25
Sparse Core Ops, SparseCore 0:
  51.1 74.4 reduce-scatter.3
  219.6 71.4 reduce-scatter.5
  466.0 72.0 reduce-scatter.7
where the time goes:
time: 597 us; the launch traced here: 596 us
  blocking collectives  334 us (56%)
  waiting for transfers between devices  217 us (36%)
  matrix products  24.1 us (4%)
  between operations  13.2 us (2%)
  other arithmetic  7.54 us (1%)
    reduce_scatter x3, waiting for transfers between devices, apply_columns(): lax.psum_scatter(lax.dot_general(design_matrix, values, (((0,), (1,)), ((...  217 us
    all_gather x3, blocking collectives, apply_rows(): lax.all_gather(vector_half, 'samp', axis=1, tiled=True)  96.7 us
    psum x2, blocking collectives, precondition(): lax.psum(jnp.sum(residual * precond_res, axis=1), ('samp', 'feat'))  91.6 us
    psum x2, blocking collectives, precondition(): projected = lax.psum(projected, ('samp', 'feat'))  88.3 us
    psum x1, blocking collectives, shards(): lax.psum(jnp.sum(direction * hess_dir, axis=1), ('samp', 'feat'))  49.8 us
  transfers between devices with their start and end apart: 3, of which 3 were waited for; matrix products, arithmetic and copies ran while one was open for 0% of the time, Pallas kernels for 0%

commit v1 on v0

--- a/solution.py
+++ b/solution.py
@@ -41,7 +41,9 @@
             precision=lax.Precision.HIGHEST,
         )
         precond_res = residual + correction
-        res_dot = lax.psum(jnp.sum(residual * precond_res, axis=1), ("samp", "feat"))
+        res_dot = jnp.sum(residual * precond_res, axis=1)
+        for src_i in ("feat", "samp"):
+            res_dot = jax.lax.psum(res_dot, src_i)
         return (precond_res, res_dot)
 
     logits = apply_rows(weights)

time: 597 us -> 637 us (1.067)
  blocking collectives: 334 us -> 374 us
    psum x1 -> x2, blocking collectives: 49.8 us -> 99.4 us  [shards(): lax.psum(jnp.sum(direction * hess_dir, axis=1), ('samp', 'feat'))]
    psum x2 -> x4, blocking collectives: 91.6 us -> 63.1 us  [precondition(): res_dot = jax.lax.psum(res_dot, src_i)]
    psum x2, blocking collectives: 88.3 us -> 98 us  [precondition(): projected = lax.psum(projected, ('samp', 'feat'))]
    all_gather x3, blocking collectives: 96.7 us -> 106 us  [apply_rows(): lax.all_gather(vector_half, 'samp', axis=1, tiled=True)]
where the time goes in v1:
time: 637 us; the launch traced here: 636 us
  blocking collectives  374 us (59%)
  waiting for transfers between devices  216 us (34%)
  matrix products  24.1 us (4%)
  between operations  13.2 us (2%)
  other arithmetic  7.54 us (1%)
    reduce_scatter x3, waiting for transfers between devices, apply_columns(): lax.psum_scatter(lax.dot_general(design_matrix, values, (((0,), (1,)), ((...  216 us
    all_gather x3, blocking collectives, apply_rows(): lax.all_gather(vector_half, 'samp', axis=1, tiled=True)  106 us
    psum x2, blocking collectives, shards(): lax.psum(jnp.sum(direction * hess_dir, axis=1), ('samp', 'feat'))  99.4 us
    psum x2, blocking collectives, precondition(): projected = lax.psum(projected, ('samp', 'feat'))  98 us
    psum x4, blocking collectives, precondition(): res_dot = jax.lax.psum(res_dot, src_i)  63.1 us
  transfers between devices with their start and end apart: 3, of which 3 were waited for; matrix products, arithmetic and copies ran while one was open for 0% of the time, Pallas kernels for 0%

profile of v1, /device:TPU:10, one launch (start us, length us, event | category | flops | bytes accessed | tf_op | source)
XLA Modules:
  0.0 635.8 jit_solution(2719334111356953145)
XLA Ops:
  6.5 0.0 copy-start
  6.5 0.0 reduce-scatter.4.cloned.1.call-start
  6.5 0.7 convert_element_type.24
  7.3 0.8 convert_element_type.23
  8.1 33.0 %all_gather.9 = bf16[16,16384]{1,0:T(8,128)(2,1)S(1)} all-gather(bf16[16,1024]{1,0:T(8,128)(2,1)S(1)} %convert_element_type.23), channel_id=1, replica_groups=mesh['samp'=16,'feat'=2] {'samp'}, dimensions={1}, use_global_device_ids=true | all-gather | bytes 557056 | tf_op jit(solution)/shard_map/all_gather | solution.py:17
  41.1 3.4 fusion.22
  44.4 0.0 copy-start.3
  44.4 0.0 copy-start.2
  44.4 0.0 copy-start.1
  44.5 2.6 psum.77
  47.1 3.8 convolution_bitcast_fusion.2
  51.0 0.0 reduce-scatter.4.cloned.1.call-update
  51.0 0.0 reduce-scatter.6.cloned.1.call-start
  51.0 0.0 copy-done.3
  51.0 0.6 reduce_min.9
  51.6 0.0 copy-done.2
  51.6 0.6 broadcast_add_fusion
  52.3 73.3 %reduce-scatter.4.cloned.1.call-done = f32[1024,16]{0,1:T(8,128)} async-done(((f32[16384,16]{0,1:T(8,128)}), f32[1024,16]{0,1:T(8,128)}) %reduce-scatter.4.cloned.1.call-update) | async-done | bytes 65552 | tf_op jit(solution)/shard_map/reduce_scatter | solution.py:25
  125.6 0.0 copy-done.1
  125.6 0.9 fusion.2
  126.6 0.0 copy-done
  126.6 0.4 fusion.23
  127.0 50.1 %psum.78 = f32[16,384]{1,0:T(8,128)S(1)} all-reduce(f32[16,384]{1,0:T(8,128)S(1)} %fusion.23), channel_id=1, replica_groups=mesh['samp'=16,'feat'=2] {'samp','feat'}, use_global_device_ids=true, to_apply=%region_3.0 | all-reduce | flops 6144 | bytes 49152 | tf_op jit(solution)/shard_map/psum | solution.py:36
  177.1 0.7 fusion.21
  177.8 32.0 %all_gather.10 = bf16[16,16384]{1,0:T(8,128)(2,1)S(1)} all-gather(bf16[16,1024]{1,0:T(8,128)(2,1)S(1)} %get-tuple-element.7), channel_id=1, replica_groups=mesh['samp'=16,'feat'=2] {'samp'}, dimensions={1}, use_global_device_ids=true | all-gather | bytes 557056 | tf_op jit(solution)/shard_map/all_gather | solution.py:17
  209.8 3.4 fusion.24
  213.1 2.5 psum.81
  215.6 3.8 convolution_bitcast_fusion.1
  219.5 0.0 reduce-scatter.6.cloned.1.call-update
  219.5 0.0 reduce-scatter.8.cloned.1.call-start
  219.5 71.6 %reduce-scatter.6.cloned.1.call-done = f32[1024,16]{0,1:T(8,128)} async-done(((f32[16384,16]{0,1:T(8,128)}), f32[1024,16]{0,1:T(8,128)}) %reduce-scatter.6.cloned.1.call-update) | async-done | bytes 65552 | tf_op jit(solution)/shard_map/reduce_scatter | solution.py:25
  291.1 1.0 multiply_reduce_fusion.1
  292.1 49.7 %psum.82 = f32[16]{0:T(128)S(1)} all-reduce(f32[16]{0:T(128)S(1)} %get-tuple-element.5), channel_id=1, replica_groups=mesh['samp'=16,'feat'=2] {'samp','feat'}, use_global_device_ids=true, to_apply=%region_10.0 | all-reduce | flops 16 | bytes 128 | tf_op jit(solution)/shard_map/psum | solution.py:64
  341.8 2.4 psum.79
  344.3 29.1 %psum.80 = f32[16]{0:T(128)S(1)} all-reduce(f32[16]{0:T(128)S(1)} %psum.79), channel_id=1, replica_groups=mesh['samp'=16,'feat'=2] {'samp'}, use_global_device_ids=true, to_apply=%region_6.0 | all-reduce | flops 16 | bytes 128 | tf_op jit(solution)/shard_map/psum | solution.py:46
  373.4 0.9 multiply_subtract_fusion
  374.3 0.4 fusion.25
  374.8 47.9 %psum.83 = f32[16,384]{1,0:T(8,128)S(1)} all-reduce(f32[16,384]{1,0:T(8,128)S(1)} %fusion.25), channel_id=1, replica_groups=mesh['samp'=16,'feat'=2] {'samp','feat'}, use_global_device_ids=true, to_apply=%region_11.0 | all-reduce | flops 6144 | bytes 49152 | tf_op jit(solution)/shard_map/psum | solution.py:36
  422.7 0.8 multiply_reduce_fusion
  423.5 2.5 psum.84
  426.0 29.1 %psum.85 = f32[16]{0:T(128)S(1)} all-reduce(f32[16]{0:T(128)S(1)} %psum.84), channel_id=1, replica_groups=mesh['samp'=16,'feat'=2] {'samp'}, use_global_device_ids=true, to_apply=%region_14.0 | all-reduce | flops 16 | bytes 128 | tf_op jit(solution)/shard_map/psum | solution.py:46
  455.1 0.1 fusion.20
  455.2 41.4 %all_gather.11 = bf16[16,16384]{1,0:T(8,128)(2,1)S(1)} all-gather(bf16[16,1024]{1,0:T(8,128)(2,1)S(1)} %fusion.20), channel_id=1, replica_groups=mesh['samp'=16,'feat'=2] {'samp'}, dimensions={1}, use_global_device_ids=true | all-gather | bytes 557056 | tf_op jit(solution)/shard_map/all_gather | solution.py:17
  496.6 3.4 fusion.26
  500.0 2.5 psum.86
  502.5 3.9 convolution_bitcast_fusion
  506.3 0.0 reduce-scatter.8.cloned.1.call-update
  506.3 71.5 %reduce-scatter.8.cloned.1.call-done = f32[1024,16]{0,1:T(8,128)} async-done(((f32[16384,16]{0,1:T(8,128)}), f32[1024,16]{0,1:T(8,128)}) %reduce-scatter.8.cloned.1.call-update) | async-done | bytes 65552 | tf_op jit(solution)/shard_map/reduce_scatter | solution.py:25
  577.8 1.0 fusion.1
  578.9 49.7 %psum.87 = f32[16]{0:T(128)S(1)} all-reduce(f32[16]{0:T(128)S(1)} %fusion.1), channel_id=1, replica_groups=mesh['samp'=16,'feat'=2] {'samp','feat'}, use_global_device_ids=true, to_apply=%region_18.0 | all-reduce | flops 16 | bytes 128 | tf_op jit(solution)/shard_map/psum | solution.py:64
  628.6 0.7 add_add_fusion
  (3 shorter events, 0.0 us)
Async XLA Ops:
  6.5 120.0 %copy-start = (bf16[1024,384]{1,0:T(8,128)(2,1)S(1)}, bf16[1024,384]{1,0:T(8,128)(2,1)}, u32[]{:S(2)}) copy-start(bf16[1024,384]{1,0:T(8,128)(2,1)} %param.10) | copy-start | bytes 2359300
  6.5 119.1 %reduce-scatter.4.cloned.1.call-start = ((), (), s32[]{:S(2)}) async-start(), calls=%async_computation.3 | async-start | bytes 1114112 | tf_op jit(solution)/shard_map/reduce_scatter | solution.py:25
  44.4 6.6 %copy-start.3 = (f32[384]{0:T(512)S(1)}, f32[384]{0:T(512)}, u32[]{:S(2)}) copy-start(f32[384]{0:T(512)} %param.11) | copy-start | bytes 4612
  44.4 7.2 %copy-start.2 = (f32[16]{0:T(128)S(1)}, f32[16]{0:T(128)}, u32[]{:S(2)}) copy-start(f32[16]{0:T(128)} %param.9) | copy-start | bytes 196
  44.4 81.2 %copy-start.1 = (f32[16,1024]{1,0:T(8,128)S(1)}, f32[16,1024]{1,0:T(8,128)}, u32[]{:S(2)}) copy-start(f32[16,1024]{1,0:T(8,128)} %param.8) | copy-start | bytes 196612
  51.0 240.1 %reduce-scatter.6.cloned.1.call-start = ((), (), s32[]{:S(2)}) async-start(), calls=%async_computation.4 | async-start | bytes 1114112 | tf_op jit(solution)/shard_map/reduce_scatter | solution.py:25
  219.5 358.3 %reduce-scatter.8.cloned.1.call-start = ((), (), s32[]{:S(2)}) async-start(), calls=%async_computation.5 | async-start | bytes 1114112 | tf_op jit(solution)/shard_map/reduce_scatter | solution.py:25
Sparse Core Ops, SparseCore 0:
  51.1 74.4 reduce-scatter.3
  219.6 71.4 reduce-scatter.5
  506.4 71.3 reduce-scatter.7
